TPU v7x, 32 devices: a whole 2x2x4 slice. The times are simulated.
32 devices in a mesh: vocab: 8 (over z, x), dp: 4 (over y, core).
Axes of the slice: x: 2, y: 2, z: 4, core: 2. Of those that a mesh axis runs over, the one named last changes fastest.
Arguments:
- out_grads: float32 [4096, 4096], P(('vocab', 'dp')), may hold values from -6 to 6
- token_ids: int32 [4096], P(('vocab', 'dp')), may hold values from 0 to 128255, as said below
Outputs:
- table_grad: bfloat16 [128256, 4096], P('vocab', 'dp')
Inputs may be any that keep to these rules, and one draw needn't show every extreme that they name: `token_ids`: call ids k * 16032 to (k + 1) * 16032 - 1 block k. The 128 tokens of one device hold at most 48 ids of any one block; one block, the same for all devices, holds exactly 48 ids of every device.
All inputs are finite; a program needn't handle non-finite values.
Results may differ from a plain program's by a relative error of at most 0.001.
Values sent between devices are 32-bit elements; how exact they have to be, the bound alone decides.
A program may use at most 192 MiB of HBM per device.

v0:
```python
import jax
import jax.numpy as jnp
from jax import lax
from jax.sharding import PartitionSpec as P

VOCAB = 128256


def slot_tables(token_ids, rows_own, owners, capacity):
    tok_count = token_ids.shape[0]
    owner_of = token_ids // rows_own
    local_row = token_ids - owner_of * rows_own
    positions = lax.iota(jnp.int32, tok_count)
    earlier = (owner_of[:, None] == owner_of[None, :]) & (positions[None, :] < positions[:, None])
    slot_of = jnp.sum(earlier.astype(jnp.int32), axis=1)
    owner_ids = lax.iota(jnp.int32, owners)
    slot_ids = lax.iota(jnp.int32, capacity)
    matches = (owner_of[None, None, :] == owner_ids[:, None, None]) & (
        slot_of[None, None, :] == slot_ids[None, :, None]
    )
    filled = jnp.any(matches, axis=2)
    token_at = jnp.where(
        filled, jnp.sum(jnp.where(matches, positions[None, None, :], 0), axis=2), -1
    )
    row_at = jnp.where(filled, jnp.sum(jnp.where(matches, local_row[None, None, :], 0), axis=2), 0)
    return (token_at, row_at)


def local(out_grads, token_ids):
    owners = lax.axis_size("vocab")
    tok_count = token_ids.shape[0]
    rows_own = VOCAB // owners
    capacity = 3 * tok_count // owners
    token_at, row_at = slot_tables(token_ids, rows_own, owners, capacity)
    token_cols = lax.all_to_all(out_grads, "dp", split_axis=1, concat_axis=0, tiled=True)
    token_all, row_all = (
        lax.all_gather(token_at, "dp", axis=1, tiled=True),
        lax.all_gather(row_at, "dp", axis=1, tiled=True),
    )
    source = lax.broadcasted_iota(jnp.int32, token_all.shape, 1) // capacity
    index = source * tok_count + jnp.maximum(token_all, 0)
    picked = jnp.take(token_cols, index, axis=0)
    outgoing = jnp.where((token_all >= 0)[:, :, None], picked, 0.0)
    arrived, arrived_rows = (
        lax.all_to_all(outgoing, "vocab", split_axis=0, concat_axis=0, tiled=True),
        lax.all_to_all(row_all, "vocab", split_axis=0, concat_axis=0, tiled=True),
    )
    columns = arrived.reshape(-1, arrived.shape[2])
    row_index = arrived_rows.reshape(-1)
    table_sum = jax.ops.segment_sum(columns, row_index, num_segments=rows_own)
    return table_sum.astype(jnp.bfloat16)


def solution(mesh):
    in_specs = (P(("vocab", "dp"), None), P(("vocab", "dp")))
    out_specs = P("vocab", "dp")
    return jax.shard_map(local, mesh=mesh, in_specs=in_specs, out_specs=out_specs, check_vma=False)
```

profile of v0, /device:TPU:0, one launch (start us, length us, event | category | flops | bytes accessed | tf_op | source)
XLA Modules:
  0.0 485.5 jit_solution(397709826431588105)
XLA Ops:
  0.0 0.0 copy-start
  0.0 3.2 copy.19
  3.2 4.3 all-to-all-start.1
  7.4 0.0 copy-done
  7.5 0.2 convert_reduce_fusion
  7.7 0.2 and_reduce_fusion
  7.9 0.4 fusion.1
  8.3 25.9 %all-gather.1 = s32[4,48,8]{1,2,0:T(8,128)S(1)} all-gather(s32[1,48,8]{1,2,0:T(8,128)S(1)} %get-tuple-element.11), channel_id=1, replica_groups=mesh['vocab'=8,'dp'=4] {'dp'}, dimensions={0}, use_global_device_ids=true | all-gather | bytes 7680 | tf_op jit(solution)/shard_map/all_gather | solution.py:37
  34.1 0.1 reshape.91
  34.2 0.1 reshape.89
  34.4 0.1 reshape.67
  34.4 5.2 %all-gather = s32[4,48,8]{1,2,0:T(8,128)S(1)} all-gather(s32[1,48,8]{1,2,0:T(8,128)S(1)} %get-tuple-element.12), channel_id=1, replica_groups=mesh['vocab'=8,'dp'=4] {'dp'}, dimensions={0}, use_global_device_ids=true | all-gather | bytes 7680 | tf_op jit(solution)/shard_map/all_gather | solution.py:38
  39.6 0.1 reshape.85
  39.7 0.6 copy.13
  40.3 0.0 all-to-all-done.1
  40.3 6.6 %all-to-all-start = ((s32[8,1,192]{2,1,0:T(1,128)}), s32[8,1,192]{2,1,0:T(1,128)S(1)}, u32[]{:S(2)}, u32[]{:S(2)}) async-start(s32[8,1,192]{2,1,0:T(1,128)} %copy.13), calls=%async_computation | async-start | bytes 16384 | tf_op jit(solution)/shard_map/all_to_all | solution.py:46
  46.9 5.7 %gather_fusion = f32[1536,1024]{1,0:T(8,128)} fusion(f32[512,1024]{1,0:T(8,128)S(1)} %bitcast.32, s32[2048]{0:T(1024)S(1)} %pad_clamp_fusion), kind=kCustom, calls=%fused_computation | custom fusion | bytes 12589056 | tf_op jit(solution)/shard_map/jit(_take)/gather | solution.py:42
  52.7 5.0 %select_select_fusion = f32[8,192,1024]{2,1,0:T(8,128)} fusion(f32[8,192,1024]{2,1,0:T(8,128)} %bitcast.33, pred[8,192]{1,0:T(8,128)(4,1)S(1)} %get-tuple-element.7, pred[8,192]{1,0:T(8,128)(4,1)S(1)} %bitcast.37), kind=kLoop, calls=%fused_computation.2 | loop fusion | flops 3145728 | bytes 12585984 | tf_op jit(solution)/shard_map/jit(_where)/select_n | solution.py:43
  57.6 0.0 all-to-all-done
  57.6 6.0 %all-to-all-start.2 = ((f32[8,192,1024]{2,1,0:T(8,128)}), f32[8,192,1024]{2,1,0:T(8,128)}, u32[]{:S(2)}, u32[]{:S(2)}) async-start(f32[8,192,1024]{2,1,0:T(8,128)} %select_select_fusion), calls=%async_computation.2 | async-start | bytes 12582912 | tf_op jit(solution)/shard_map/all_to_all | solution.py:45
  63.7 0.1 reshape.75
  63.7 138.1 %all-to-all-done.2 = f32[8,192,1024]{2,1,0:T(8,128)} async-done(((f32[8,192,1024]{2,1,0:T(8,128)}), f32[8,192,1024]{2,1,0:T(8,128)}, u32[]{:S(2)}, u32[]{:S(2)}) %all-to-all-start.2) | async-done | bytes 6291488 | tf_op jit(solution)/shard_map/all_to_all | solution.py:45
  201.8 20.7 %broadcast_in_dim.63 = f32[16032,1024]{1,0:T(8,128)} broadcast(f32[]{:T(128)} %constant.18.clone.1), dimensions={} | broadcast | bytes 65667076 | tf_op jit(solution)/shard_map/broadcast_in_dim | solution.py:50
  222.5 231.1 %scatter_fusion = f32[16032,1024]{1,0:T(8,128)} fusion(f32[16032,1024]{1,0:T(8,128)} %broadcast_in_dim.63, s32[1536]{0:T(1024)S(1)} %reshape.75, f32[1536,1024]{1,0:T(8,128)} %bitcast.11), kind=kCustom, calls=%fused_computation.1 | custom fusion | flops 1572864 | bytes 18880512 | tf_op jit(solution)/shard_map/scatter-add | solution.py:50
  453.6 31.9 %convert_element_type.7 = bf16[16032,1024]{1,0:T(8,128)(2,1)} convert(f32[16032,1024]{1,0:T(8,128)} %scatter_fusion) | non-fusion elementwise | flops 16416768 | bytes 98500608 | tf_op jit(solution)/shard_map/convert_element_type | solution.py:51
  (14 shorter events, 0.1 us)
Async XLA Ops:
  0.0 7.4 %copy-start = (s32[128]{0:T(128)S(1)}, s32[128]{0:T(128)}, u32[]{:S(2)}) copy-start(s32[128]{0:T(128)} %param.3) | copy-start | bytes 1540
  3.2 37.2 %all-to-all-start.1 = ((f32[128,4,1024]{2,0,1:T(8,128)}), f32[128,4,1024]{2,0,1:T(8,128)S(1)}, u32[]{:S(2)}, u32[]{:S(2)}) async-start(f32[128,4,1024]{2,0,1:T(8,128)} %bitcast.34), calls=%async_computation.1 | async-start | bytes 4194304 | tf_op jit(solution)/shard_map/all_to_all | solution.py:35
  40.3 17.3 %all-to-all-start = ((s32[8,1,192]{2,1,0:T(1,128)}), s32[8,1,192]{2,1,0:T(1,128)S(1)}, u32[]{:S(2)}, u32[]{:S(2)}) async-start(s32[8,1,192]{2,1,0:T(1,128)} %copy.13), calls=%async_computation | async-start | bytes 16384 | tf_op jit(solution)/shard_map/all_to_all | solution.py:46
  57.6 144.2 %all-to-all-start.2 = ((f32[8,192,1024]{2,1,0:T(8,128)}), f32[8,192,1024]{2,1,0:T(8,128)}, u32[]{:S(2)}, u32[]{:S(2)}) async-start(f32[8,192,1024]{2,1,0:T(8,128)} %select_select_fusion), calls=%async_computation.2 | async-start | bytes 12582912 | tf_op jit(solution)/shard_map/all_to_all | solution.py:45
where the time goes:
time: 493 us; the launch traced here: 485 us
  other arithmetic  269 us (55%)
  waiting for transfers between devices  138 us (28%)
  blocking collectives  31.1 us (6%)
  local copies, waits for them, and re-layouts  30.6 us (6%)
  starting transfers between devices  16.9 us (3%)
    scatter-add x1, other arithmetic, local(): table_sum = jax.ops.segment_sum(columns, row_index, num_segments=rows_own)  231 us
    all_to_all x1, waiting for transfers between devices, local(): lax.all_to_all(outgoing, 'vocab', split_axis=0, concat_axis=0, tiled=True)  138 us
    convert_element_type x1, other arithmetic, local(): return table_sum.astype(jnp.bfloat16)  31.9 us
    all_gather x1, blocking collectives, local(): lax.all_gather(token_at, 'dp', axis=1, tiled=True)  25.9 us
    broadcast_in_dim x1, local copies, waits for them, and re-layouts, local(): table_sum = jax.ops.segment_sum(columns, row_index, num_segments=rows_own)  20.7 us
  transfers between devices with their start and end apart: 3, of which 1 were waited for; matrix products, arithmetic and copies ran while one was open for 3% of the time, Pallas kernels for 0%

commit v1 on v0

v1 whole, which is shorter than its diff:
```python
import functools

import jax
import jax.numpy as jnp
from jax import lax
from jax.experimental import pallas as pl
from jax.experimental.pallas import tpu as pltpu
from jax.sharding import PartitionSpec as P

VOCAB = 128256


def ranks_in_block(owner_of):
    positions = lax.iota(jnp.int32, owner_of.shape[1])
    earlier = (owner_of[:, :, None] == owner_of[:, None, :]) & (positions[None, None, :] < positions[None, :, None])
    return jnp.sum(earlier.astype(jnp.int32), axis=2)


def table_kernel(tile, slots_ref, rows_ref, starts_ref, data_ref, out_ref, acc):
    step = pl.program_id(0)
    base = step * tile
    acc[...] = jnp.zeros_like(acc)

    @pl.loop(starts_ref[step], starts_ref[step + 1])
    def _(at):
        row = rows_ref[at] - base
        slot = slots_ref[at]
        acc[pl.ds(row, 1), :] += data_ref[pl.ds(slot, 1), :]

    out_ref[...] = acc[...].astype(out_ref.dtype)


def build_table(data, slots, rows, starts, rows_own, tile):
    count, width = data.shape
    tiles = pl.cdiv(rows_own, tile)
    return pl.pallas_call(
        functools.partial(table_kernel, tile),
        out_shape=jax.ShapeDtypeStruct((rows_own, width), jnp.bfloat16),
        grid_spec=pltpu.PrefetchScalarGridSpec(
            num_scalar_prefetch=3,
            grid=(tiles,),
            in_specs=[pl.BlockSpec((count, width), lambda i, *_: (0, 0), pipeline_mode=pl.Buffered(1))],
            out_specs=pl.BlockSpec((tile, width), lambda i, *_: (i, 0)),
            scratch_shapes=[pltpu.VMEM((tile, width), jnp.float32)],
        ),
        compiler_params=pltpu.CompilerParams(vmem_limit_bytes=40 * 2**20),
        name="table",
    )(slots, rows, starts, data)


def order_slots(ids_all, block, rows_own, capacity, tile):
    devices = ids_all.shape[0]
    mine = (ids_all // rows_own) == block
    positions = lax.iota(jnp.int32, ids_all.shape[1])
    before = mine[:, None, :] & (positions[None, None, :] < positions[None, :, None])
    rank = jnp.sum(before.astype(jnp.int32), axis=2)
    slot_ids = lax.iota(jnp.int32, capacity)
    hit = mine[:, None, :] & (rank[:, None, :] == slot_ids[None, :, None])
    local_row = ids_all - block * rows_own
    row_at = jnp.sum(jnp.where(hit, local_row[:, None, :] + 1, 0), axis=2) - 1
    row_at = row_at.reshape(-1)
    total = devices * capacity
    slots = lax.iota(jnp.int32, total)
    key = jnp.where(row_at >= 0, row_at, rows_own) * total + slots
    place = jnp.sum((key[None, :] < key[:, None]).astype(jnp.int32), axis=1)
    sorted_key = jnp.sum(jnp.where(place[None, :] == slots[:, None], key[None, :], 0), axis=1)
    sorted_row = sorted_key // total
    sorted_slot = sorted_key - sorted_row * total
    tiles = pl.cdiv(rows_own, tile)
    bounds = jnp.minimum(lax.iota(jnp.int32, tiles + 1) * tile, rows_own)
    row_key = key // total
    starts = jnp.sum((row_key[None, :] < bounds[:, None]).astype(jnp.int32), axis=1)
    return sorted_slot, sorted_row, starts


def local(out_grads, token_ids):
    owners, dp = lax.axis_size("vocab"), lax.axis_size("dp")
    tok_count, width = out_grads.shape
    rows_own = VOCAB // owners
    capacity = 3 * tok_count // owners
    tile = 1024
    ids_all = lax.all_gather(token_ids, ("vocab", "dp"), axis=0, tiled=False)
    owner_of = token_ids // rows_own
    rank = ranks_in_block(owner_of[None])[0]
    target = owner_of * capacity + rank
    pick = (target[None, :] == lax.iota(jnp.int32, owners * capacity)[:, None]).astype(jnp.float32)
    outgoing = jnp.dot(pick, out_grads, precision=lax.Precision.HIGHEST)
    outgoing = outgoing.reshape(owners, capacity, dp, width // dp).transpose(0, 2, 1, 3)
    outgoing = outgoing.reshape(owners * dp, capacity, width // dp)
    arrived = lax.all_to_all(outgoing, ("vocab", "dp"), split_axis=0, concat_axis=0, tiled=True)
    slots, rows, starts = order_slots(ids_all, lax.axis_index("vocab"), rows_own, capacity, tile)
    data = arrived.reshape(owners * dp * capacity, width // dp)
    return build_table(data, slots, rows, starts, rows_own, tile)


def solution(mesh):
    in_specs = (P(("vocab", "dp"), None), P(("vocab", "dp")))
    out_specs = P("vocab", "dp")
    return jax.shard_map(local, mesh=mesh, in_specs=in_specs, out_specs=out_specs, check_vma=False)
```

time: 493 us -> 229 us (0.46)
  the two profiles are of different devices: /device:TPU:0 before, /device:TPU:31 now
where the time goes in v1:
time: 229 us; the launch traced here: 227 us
  blocking collectives  161 us (70%)
  Pallas kernels  31.3 us (14%)
  local copies, waits for them, and re-layouts  17.6 us (8%)
  other arithmetic  6.56 us (3%)
  starting transfers between devices  6.17 us (3%)
  matrix products  4.54 us (2%)
    all_gather x1, blocking collectives, local(): ids_all = lax.all_gather(token_ids, ('vocab', 'dp'), axis=0, tiled=False)  161 us
    pallas_call x1, Pallas kernels, build_table(): pl.pallas_call(functools.partial(table_kernel, tile), out_shape=jax.Shape...  31.3 us
    transpose x1, local copies, waits for them, and re-layouts, local(): outgoing.reshape(owners, capacity, dp, width // dp).transpose(0, 2, 1, 3)  9.04 us
    reshape x1, local copies, waits for them, and re-layouts, local(): outgoing.reshape(owners, capacity, dp, width // dp).transpose(0, 2, 1, 3)  8.45 us
    all_to_all x1, starting transfers between devices, local(): lax.all_to_all(outgoing, ('vocab', 'dp'), split_axis=0, concat_axis=0, ti...  6.17 us
  transfers between devices with their start and end apart: 1, of which 0 were waited for; matrix products, arithmetic and copies ran while one was open for 2% of the time, Pallas kernels for 0%

profile of v1, /device:TPU:31, one launch (start us, length us, event | category | flops | bytes accessed | tf_op | source)
XLA Modules:
  0.0 227.3 jit_solution(13550693034274030116)
XLA Ops:
  0.0 0.0 copy-start
  0.0 0.8 and_select_fusion
  0.8 0.2 convert_reduce_fusion.3
  1.0 0.7 multiply_add_fusion
  1.7 0.0 copy-done
  1.7 4.5 %fusion.1 = f32[384,4096]{1,0:T(8,128)} fusion(f32[128,4096]{1,0:T(8,128)S(1)} %copy-done, s32[128]{0:T(128)S(1)} %multiply_add_fusion), kind=kOutput, calls=%fused_computation.8 | convolution fusion | flops 2415968256 | bytes 8389120 | tf_op jit(solution)/shard_map/dot_general | solution.py:87
  6.2 8.4 %reshape.147 = f32[8,48,4,1024]{3,2,1,0:T(4,128)} reshape(f32[384,4096]{1,0:T(8,128)} %fusion.1) | data formatting | bytes 12582912 | tf_op jit(solution)/shard_map/reshape | solution.py:88
  14.7 9.0 %copy.17 = f32[8,4,48,1024]{3,2,1,0:T(8,128)} copy(f32[8,4,48,1024]{3,1,2,0:T(4,128)} %bitcast.17) | data formatting | bytes 12582912 | tf_op jit(solution)/shard_map/transpose | solution.py:88
  23.7 0.0 copy-start.1
  23.7 6.2 %all-to-all-start = ((f32[32,48,1024]{2,1,0:T(8,128)}), f32[32,48,1024]{2,1,0:T(8,128)}, u32[]{:S(2)}, u32[]{:S(2)}) async-start(f32[32,48,1024]{2,1,0:T(8,128)} %bitcast.16), calls=%async_computation | async-start | bytes 12582912 | tf_op jit(solution)/shard_map/all_to_all | solution.py:90
  29.9 0.0 copy-done.1
  29.9 161.0 %all-gather.1 = s32[32,1,128]{2,1,0:T(1,128)S(1)} all-gather(s32[1,1,128]{2,1,0:T(1,128)S(1)} %bitcast.22), channel_id=2, replica_groups=mesh['vocab'=8,'dp'=4] {'vocab','dp'}, dimensions={0}, use_global_device_ids=true | all-gather | bytes 16896 | tf_op jit(solution)/shard_map/all_gather | solution.py:82
  190.9 1.3 div.31
  192.3 0.6 convert_reduce_fusion.1
  192.9 0.6 select_reduce_fusion.1
  193.5 0.1 sub.41
  193.7 0.2 convert_reduce_fusion.2.starts_ref
  193.9 1.1 convert_reduce_fusion
  194.9 1.0 select_reduce_fusion
  196.0 0.0 all-to-all-done
  196.0 31.3 %table.1 = bf16[16032,1024]{1,0:T(8,128)(2,1)} custom-call(s32[1536]{0:T(1024)S(1)} %get-tuple-element.8.slots_ref, s32[1536]{0:T(1024)S(1)} %get-tuple-element.7.rows_ref, s32[17]{0:T(128)S(1)} %convert_reduce_fusion.2.starts_ref, f32[1536,1024]{1,0:T(8,128)} %bitcast.10.data_ref), custom_call_target="tpu_custom_call" | custom-call | tf_op jit(solution)/shard_map/table/pallas_call | solution.py:36
  (8 shorter events, 0.1 us)
Async XLA Ops:
  0.0 1.7 copy-start
  23.7 6.2 %copy-start.1 = (s32[128]{0:T(128)S(1)}, s32[128]{0:T(128)}, u32[]{:S(2)}) copy-start(s32[128]{0:T(128)} %param.3) | copy-start | bytes 1540
  23.7 172.3 %all-to-all-start = ((f32[32,48,1024]{2,1,0:T(8,128)}), f32[32,48,1024]{2,1,0:T(8,128)}, u32[]{:S(2)}, u32[]{:S(2)}) async-start(f32[32,48,1024]{2,1,0:T(8,128)} %bitcast.16), calls=%async_computation | async-start | bytes 12582912 | tf_op jit(solution)/shard_map/all_to_all | solution.py:90
